TPU v7x, 32 devices: a whole 2x2x4 slice. The times are simulated.
32 devices in a mesh: seq: 16 (over z, y, core), fsdp: 2 (over x).
Axes of the slice: x: 2, y: 2, z: 4, core: 2. Of those that a mesh axis runs over, the one named last changes fastest.
Arguments:
- tokens: bfloat16 [8192, 5376], P(('seq', 'fsdp')), may hold values from -6 to 6
- norm_gain: float32 [5376], replicated, may hold values from 0.1 to 1.9
- query_weight: bfloat16 [5376, 2048], P('seq', 'fsdp'), may hold values from -0.078125 to 0.078125
- key_matrix: bfloat16 [5376, 1024], P('seq', 'fsdp'), may hold values from -0.078125 to 0.078125
- value_matrix: bfloat16 [5376, 1024], P('seq', 'fsdp'), may hold values from -0.078125 to 0.078125
- out_weight: bfloat16 [5376, 2048], P('seq', 'fsdp'), may hold values from -0.125 to 0.125
- query_gain: float32 [128], replicated, may hold values from 0.1 to 1.9
- key_gain: float32 [128], replicated, may hold values from 0.1 to 1.9
- post_gain: float32 [5376], replicated, may hold values from 0.1 to 1.9
Outputs:
- layer_out: bfloat16 [8192, 5376], P(('seq', 'fsdp'))
All inputs are finite; a program needn't handle non-finite values.
Results may differ from a plain program's by a relative error of at most 0.011.
Values may be sent and summed in bfloat16 or wider, within the bound.
A program may use at most 192 MiB of HBM per device.

v0:
```python
import jax
import jax.numpy as jnp
from jax import lax
from jax.sharding import PartitionSpec as P

HEAD_SIZE = 128
WINDOW_LENGTH = 1024


epsilon = 1e-06
score_scale = 168.0 ** (-0.5)
rope_base = 10000.0
masked_score = -1e30


def passed_along(block, axis, distance):
    devices = range(lax.axis_size(axis))
    route = [(i - distance, i) for i in devices if i - distance in devices]
    return lax.ppermute(block, axis, route)


def rms_scaled(values, gain):
    mean_square = jnp.mean(values * values, axis=-1, keepdims=True)
    return values * lax.rsqrt(mean_square + epsilon) * gain


def rotary(values, positions):
    half_width = values.shape[-1] // 2
    exponents = jnp.arange(half_width, dtype=jnp.float32) * (2.0 / values.shape[-1])
    frequency = jnp.exp(-exponents * jnp.log(jnp.float32(rope_base)))
    angles = positions.astype(jnp.float32)[:, None] * frequency[None, :]
    cosine = jnp.cos(angles)[:, None, :]
    sine = jnp.sin(angles)[:, None, :]
    first_half = values[..., :half_width]
    second_half = values[..., half_width:]
    return jnp.concatenate(
        [first_half * cosine - second_half * sine, second_half * cosine + first_half * sine],
        axis=-1,
    )


def head_states(projected, gain, positions):
    shaped = projected.reshape(projected.shape[0], -1, HEAD_SIZE)
    return rotary(rms_scaled(shaped, gain), positions).astype(jnp.bfloat16)


def window_block(query_block, key_block, value_block, query_pos, key_pos):
    scores = (
        jnp.einsum("rkgd,lkd->kgrl", query_block, key_block, preferred_element_type=jnp.float32)
        * score_scale
    )
    offset = query_pos[:, None] - key_pos[None, :]
    allowed = (offset >= 0) & (offset < WINDOW_LENGTH) & (key_pos[None, :] >= 0)
    scores = jnp.where(allowed, scores, masked_score)
    highest = jnp.max(scores, axis=-1, keepdims=True)
    raised = jnp.exp(scores - highest)
    weights = (raised / jnp.sum(raised, axis=-1, keepdims=True)).astype(jnp.bfloat16)
    mixed = jnp.einsum("kgrl,lkd->rkgd", weights, value_block, preferred_element_type=jnp.float32)
    return mixed.astype(jnp.bfloat16).reshape(query_block.shape[0], -1)


def on_device(
    tokens,
    norm_gain,
    query_weight,
    key_matrix,
    value_matrix,
    out_weight,
    query_gain,
    key_gain,
    post_gain,
):
    pair_rows = lax.all_gather(tokens, "fsdp", axis=0, tiled=True)
    shard_rows = pair_rows.shape[0]
    first_row = lax.axis_index("seq") * shard_rows
    normed_input = rms_scaled(pair_rows.astype(jnp.float32), norm_gain).astype(jnp.bfloat16)
    query_width = query_weight.shape[1]
    key_width = key_matrix.shape[1]
    local_heads = key_width // HEAD_SIZE
    query_groups = query_width // key_width
    query_full, key_full, value_full, out_full = (
        lax.all_gather(query_weight, "seq", axis=0, tiled=True),
        lax.all_gather(key_matrix, "seq", axis=0, tiled=True),
        lax.all_gather(value_matrix, "seq", axis=0, tiled=True),
        lax.all_gather(out_weight, "seq", axis=0, tiled=True),
    )
    queries_raw = jnp.dot(normed_input, query_full, preferred_element_type=jnp.float32)
    keys_raw = jnp.dot(normed_input, key_full, preferred_element_type=jnp.float32)
    values_raw = jnp.dot(normed_input, value_full, preferred_element_type=jnp.float32)
    positions = first_row + jnp.arange(shard_rows, dtype=jnp.int32)
    query_states = head_states(queries_raw, query_gain, positions).reshape(
        shard_rows, local_heads, query_groups, HEAD_SIZE
    )
    keys_now = head_states(keys_raw, key_gain, positions).reshape(shard_rows, key_width)
    values_now = values_raw.astype(jnp.bfloat16)
    stacked = jnp.stack([keys_now, values_now])
    reach = min(WINDOW_LENGTH, shard_rows)
    count = WINDOW_LENGTH // reach
    received = []
    for distance in range(1, count + 1):
        received = [passed_along(stacked, "seq", distance)] + received
    window_rows = jnp.concatenate(received + [stacked], axis=1)
    key_rows = window_rows.shape[1]
    keys_window = window_rows[0].reshape(key_rows, local_heads, HEAD_SIZE)
    values_window = window_rows[1].reshape(key_rows, local_heads, HEAD_SIZE)
    key_pos = first_row - WINDOW_LENGTH + jnp.arange(key_rows, dtype=jnp.int32)
    attended = window_block(query_states, keys_window, values_window, positions, key_pos)
    partial_out = lax.dot_general(
        attended, out_full, (((1,), (1,)), ((), ())), preferred_element_type=jnp.float32
    )
    summed = lax.psum_scatter(
        partial_out.astype(jnp.bfloat16), "fsdp", scatter_dimension=0, tiled=True
    ).astype(jnp.float32)
    return (tokens.astype(jnp.float32) + rms_scaled(summed, post_gain)).astype(jnp.bfloat16)


def solution(mesh):
    in_specs = (
        P(("seq", "fsdp"), None),
        P(),
        P("seq", "fsdp"),
        P("seq", "fsdp"),
        P("seq", "fsdp"),
        P("seq", "fsdp"),
        P(),
        P(),
        P(),
    )
    out_specs = P(("seq", "fsdp"), None)
    return jax.shard_map(
        on_device, mesh=mesh, in_specs=in_specs, out_specs=out_specs, check_vma=False
    )
```

profile of v0, /device:TPU:5, one launch (start us, length us, event | category | flops | bytes accessed | tf_op | source)
XLA Modules:
  0.0 500.8 jit_solution(12760846416064115125)
XLA Ops:
  6.5 0.7 all-gather.6.cloned.1.call-update
  7.3 0.0 all-gather.8.cloned.1.call-start
  7.3 0.7 all-gather.8.cloned.1.call-update
  8.1 0.7 all-gather.10.cloned.1.call-update
  8.8 0.5 all-gather.12.cloned.1.call-update
  9.4 0.5 all-gather.14.cloned.1.call-update
  9.9 0.0 reduce-scatter.2.cloned.1.call-start
  10.0 1.0 multiply_cosine_fusion
  11.0 0.1 copy.28
  11.1 0.1 copy.27
  11.2 70.2 %all-gather.6.cloned.1.call-done = bf16[512,5376]{1,0:T(8,128)(2,1)} async-done(((bf16[256,5376]{1,0:T(8,128)(2,1)}), bf16[512,5376]{1,0:T(8,128)(2,1)}) %all-gather.6.cloned.1.call-update) | async-done | bytes 5505040 | tf_op jit(solution)/shard_map/all_gather | solution.py:73
  81.4 3.7 fusion.6
  85.2 55.6 %all-gather.8.cloned.1.call-done = bf16[5376,512]{1,0:T(8,128)(2,1)} async-done(((bf16[336,512]{1,0:T(8,128)(2,1)}), bf16[5376,512]{1,0:T(8,128)(2,1)}) %all-gather.8.cloned.1.call-update) | async-done | bytes 5505040 | tf_op jit(solution)/shard_map/all_gather | solution.py:83
  140.8 8.0 %multiply_reduce_fusion.1 = (f32[512,4]{0,1:T(4,128)S(1)}, f32[512,512]{0,1:T(8,128)S(1)}) fusion(bf16[5376,512]{1,0:T(8,128)(2,1)} %all-gather.8.cloned.1.call-done, bf16[512,5376]{1,0:T(8,128)(2,1)} %all-gather.6.cloned.1.call-done, f32[5376]{0:T(1024)S(1)} %copy-done.9, f32[512]{0:T(512)S(1)} %add_rsqrt_fusion.2), kind=kOutput, calls=%fused_computation.41 | convolution fusion | flops 2830104576 | bytes 12090368 | tf_op jit(solution)/shard_map/dot_general | solution.py:88
  148.8 0.2 multiply_multiply_fusion.1
  149.0 0.2 subtract_convert_fusion.1
  149.2 0.2 copy.40
  149.5 49.6 %all-gather.10.cloned.1.call-done = bf16[5376,512]{1,0:T(8,128)(2,1)} async-done(((bf16[336,512]{1,0:T(8,128)(2,1)}), bf16[5376,512]{1,0:T(8,128)(2,1)}) %all-gather.10.cloned.1.call-update) | async-done | bytes 5505040 | tf_op jit(solution)/shard_map/all_gather | solution.py:84
  199.1 7.2 %fusion.22 = bf16[1,512,512]{2,1,0:T(8,128)(2,1)S(1)} fusion(bf16[5376,512]{1,0:T(8,128)(2,1)} %all-gather.10.cloned.1.call-done, bf16[512,5376]{1,0:T(8,128)(2,1)} %all-gather.6.cloned.1.call-done, f32[5376]{0:T(1024)S(1)} %copy-done.9, f32[512]{0:T(512)S(1)} %add_rsqrt_fusion.2), kind=kOutput, calls=%fused_computation.37 | convolution fusion | flops 2829844480 | bytes 11557888 | tf_op jit(solution)/shard_map/dot_general | solution.py:89
  206.3 0.1 pad_maximum_fusion
  206.4 4.2 collective-permute-start.1
  210.6 2.4 collective-permute-start
  213.0 2.0 fusion.16
  215.0 38.5 %collective-permute-done.1 = bf16[2,512,512]{2,1,0:T(8,128)(2,1)S(1)} collective-permute-done((bf16[2,512,512]{2,1,0:T(8,128)(2,1)S(1)}, bf16[2,512,512]{2,1,0:T(8,128)(2,1)S(1)}, u32[]{:S(2)}, u32[]{:S(2)}) %collective-permute-start.1) | collective-permute-done | bytes 1048608 | tf_op jit(solution)/shard_map/ppermute | solution.py:19
  253.6 27.0 %collective-permute-done = bf16[2,512,512]{2,1,0:T(8,128)(2,1)} collective-permute-done((bf16[2,512,512]{2,1,0:T(8,128)(2,1)S(1)}, bf16[2,512,512]{2,1,0:T(8,128)(2,1)}, u32[]{:S(2)}, u32[]{:S(2)}) %collective-permute-start) | collective-permute-done | bytes 1048608 | tf_op jit(solution)/shard_map/ppermute | solution.py:19
  280.5 1.4 maximum_maximum_fusion
  281.9 0.2 fusion.38
  282.1 1.6 copy.41
  283.7 1.9 reshape_squeeze.7
  285.5 24.8 %all-gather.12.cloned.1.call-done = bf16[5376,1024]{1,0:T(8,128)(2,1)} async-done(((bf16[336,1024]{1,0:T(8,128)(2,1)}), bf16[5376,1024]{1,0:T(8,128)(2,1)}) %all-gather.12.cloned.1.call-update) | async-done | bytes 11010064 | tf_op jit(solution)/shard_map/all_gather | solution.py:82
  310.3 10.3 %convolution_bitcast_fusion = f32[64,8,8,128]{3,1,2,0:T(8,128)S(1)} fusion(bf16[5376,1024]{1,0:T(8,128)(2,1)} %all-gather.12.cloned.1.call-done, bf16[512,5376]{1,0:T(8,128)(2,1)} %all-gather.6.cloned.1.call-done, f32[5376]{0:T(1024)S(1)} %copy-done.9, f32[512]{0:T(512)S(1)} %add_rsqrt_fusion.2), kind=kOutput, calls=%fused_computation.31 | convolution fusion | flops 5648154624 | bytes 18635776 | tf_op jit(solution)/shard_map/dot_general | solution.py:87
  320.7 0.5 copy.44
  321.1 0.6 multiply_reduce_fusion
  321.7 0.1 copy.30
  321.9 0.1 copy.31
  322.0 0.9 multiply_multiply_fusion
  322.9 0.9 subtract_convert_fusion
  323.8 0.1 copy.33
  323.9 0.1 copy.32
  324.1 1.0 copy-done.2
  325.1 11.9 %fusion.20 = f32[4,1536,512,2]{2,1,3,0:T(8,128)} fusion(bf16[1536,4,128,1]{2,1,0,3:T(4,128)(2,1)S(1)} %bitcast.41, bf16[512,4,2,64]{3,0,2,1:T(8,128)(2,1)S(1)} %bitcast.43, bf16[512,4,2,64]{3,0,2,1:T(8,128)(2,1)S(1)} %bitcast.45), kind=kOutput, calls=%fused_computation.34 | convolution fusion | flops 1612709888 | bytes 27787264 | tf_op jit(solution)/shard_map/rkgd,lkd->kgrl/dot_general | solution.py:49
  337.0 10.4 %fusion.39 = f32[4,2,512]{2,1,0:T(2,128)S(1)} fusion(pred[512,1536]{0,1:T(8,128)(4,1)S(1)} %copy-done.5, bf16[1536,4,128,1]{2,1,0,3:T(4,128)(2,1)S(1)} %bitcast.42, bf16[512,4,2,64]{3,0,2,1:T(8,128)(2,1)S(1)} %bitcast.44, bf16[512,4,2,64]{3,0,2,1:T(8,128)(2,1)} %bitcast.46), kind=kOutput, calls=%fused_computation.65 | convolution fusion | flops 1637877248 | bytes 3424256 | tf_op jit(solution)/shard_map/sub | solution.py:56
  347.4 14.2 %fusion.17 = bf16[4,128,2,512]{3,1,2,0:T(8,128)(2,1)S(1)} fusion(bf16[1536,4,128,1]{0,2,3,1:T(8,128)(2,1)} %bitcast.48, f32[4,2,512]{2,1,0:T(2,128)S(1)} %fusion.39, f32[4,1536,512,2]{2,1,3,0:T(8,128)} %fusion.20, pred[512,1536]{0,1:T(8,128)(4,1)S(1)} %copy-done.5), kind=kOutput, calls=%fused_computation.32 | convolution fusion | flops 1642599936 | bytes 28590080 | tf_op jit(solution)/shard_map/kgrl,lkd->rkgd/dot_general | solution.py:58
  361.7 46.0 %all-gather.14.cloned.1.call-done = bf16[5376,1024]{1,0:T(8,128)(2,1)} async-done(((bf16[336,1024]{1,0:T(8,128)(2,1)}), bf16[5376,1024]{1,0:T(8,128)(2,1)}) %all-gather.14.cloned.1.call-update) | async-done | bytes 11010064 | tf_op jit(solution)/shard_map/all_gather | solution.py:85
  407.7 12.0 %convolution_convert_fusion = bf16[512,5376]{1,0:T(8,128)(2,1)} fusion(bf16[512,1024]{0,1:T(8,128)(2,1)S(1)} %bitcast.49, bf16[5376,1024]{1,0:T(8,128)(2,1)} %all-gather.14.cloned.1.call-done), kind=kOutput, calls=%fused_computation.14 | convolution fusion | flops 5639897088 | bytes 17563648 | tf_op jit(solution)/shard_map/dot_general | solution.py:108
  419.7 67.3 %reduce-scatter.2.cloned.1.call-done = bf16[256,5376]{1,0:T(8,128)(2,1)} async-done(((bf16[512,5376]{1,0:T(8,128)(2,1)}), bf16[256,5376]{1,0:T(8,128)(2,1)}) %reduce-scatter.2.cloned.1.call-update) | async-done | bytes 2752528 | tf_op jit(solution)/shard_map/reduce_scatter | solution.py:111
  487.0 2.4 fusion.9
  489.5 4.5 fusion.12
  (33 shorter events, 0.3 us)
Async XLA Ops:
  6.5 134.2 %copy-start.9 = (f32[5376]{0:T(1024)S(1)}, f32[5376]{0:T(1024)}, u32[]{:S(2)}) copy-start(f32[5376]{0:T(1024)} %param.10) | copy-start | bytes 64516
  6.5 74.9 %all-gather.6.cloned.1.call-start = ((), (), s32[]{:S(2)}) async-start(), calls=%async_computation.1 | async-start | bytes 8257536 | tf_op jit(solution)/shard_map/all_gather | solution.py:73
  7.3 133.5 %all-gather.8.cloned.1.call-start = ((), (), s32[]{:S(2)}) async-start(), calls=%async_computation.2 | async-start | bytes 5849088 | tf_op jit(solution)/shard_map/all_gather | solution.py:83
  8.0 191.1 %all-gather.10.cloned.1.call-start = ((), (), s32[]{:S(2)}) async-start(), calls=%async_computation.3 | async-start | bytes 5849088 | tf_op jit(solution)/shard_map/all_gather | solution.py:84
  8.7 301.6 %all-gather.12.cloned.1.call-start = ((), (), s32[]{:S(2)}) async-start(), calls=%async_computation.4 | async-start | bytes 11698176 | tf_op jit(solution)/shard_map/all_gather | solution.py:82
  9.3 398.3 %all-gather.14.cloned.1.call-start = ((), (), s32[]{:S(2)}) async-start(), calls=%async_computation.5 | async-start | bytes 11698176 | tf_op jit(solution)/shard_map/all_gather | solution.py:85
  9.9 477.1 %reduce-scatter.2.cloned.1.call-start = ((), (), s32[]{:S(2)}) async-start(), calls=%async_computation.6 | async-start | bytes 8257536 | tf_op jit(solution)/shard_map/reduce_scatter | solution.py:111
  11.0 137.8 %copy-start.3 = (f32[512,64]{1,0:T(8,128)}, f32[512,64]{1,0:T(8,128)S(1)}, u32[]{:S(2)}) copy-start(f32[512,64]{1,0:T(8,128)S(1)} %get-tuple-element.12) | copy-start | bytes 393220
  85.2 63.7 %copy-start.7 = (f32[128]{0:T(128)S(1)}, f32[128]{0:T(128)}, u32[]{:S(2)}) copy-start(f32[128]{0:T(128)} %param.16) | copy-start | bytes 1540
  206.4 47.1 %collective-permute-start.1 = (bf16[2,512,512]{2,1,0:T(8,128)(2,1)S(1)}, bf16[2,512,512]{2,1,0:T(8,128)(2,1)S(1)}, u32[]{:S(2)}, u32[]{:S(2)}) collective-permute-start(bf16[2,512,512]{2,1,0:T(8,128)(2,1)S(1)} %pad_maximum_fusion), channel_id=1, source_target_pairs={{0,2},{2,4},{4,6},{6,8},{8,10},{10,12},{12,14},{14,16},{16,18},{18... | collective-permute-start | bytes 3145736 | tf_op jit(solution)/shard_map/ppermute | solution.py:19
  210.6 69.9 %collective-permute-start = (bf16[2,512,512]{2,1,0:T(8,128)(2,1)S(1)}, bf16[2,512,512]{2,1,0:T(8,128)(2,1)}, u32[]{:S(2)}, u32[]{:S(2)}) collective-permute-start(bf16[2,512,512]{2,1,0:T(8,128)(2,1)S(1)} %pad_maximum_fusion), channel_id=1, source_target_pairs={{0,4},{2,6},{4,8},{6,10},{8,12},{10,14},{12,16},{14,18},{16,20},{1... | collective-permute-start | bytes 3145736 | tf_op jit(solution)/shard_map/ppermute | solution.py:19
  320.6 1.4 copy-start.8
  320.6 2.2 copy-start.4
  322.9 2.2 copy-start.1
  324.0 1.0 copy-start.2
  325.1 12.0 %copy-start.5 = (pred[512,1536]{0,1:T(8,128)(4,1)S(1)}, pred[512,1536]{0,1:T(8,128)(4,1)}, u32[]{:S(2)}) copy-start(pred[512,1536]{0,1:T(8,128)(4,1)} %fusion.16) | copy-start | bytes 2359300
  419.7 69.8 %copy-start = (bf16[256,5376]{1,0:T(8,128)(2,1)S(1)}, bf16[256,5376]{1,0:T(8,128)(2,1)}, u32[]{:S(2)}) copy-start(bf16[256,5376]{1,0:T(8,128)(2,1)} %param.9) | copy-start | bytes 8257540
  419.7 69.8 %copy-start.6 = (f32[5376]{0:T(1024)S(1)}, f32[5376]{0:T(1024)}, u32[]{:S(2)}) copy-start(f32[5376]{0:T(1024)} %param.17) | copy-start | bytes 64516
Sparse Core Ops, SparseCore 0:
  8.9 72.5 all-gather.5
  83.7 57.0 all-gather.7
  143.1 55.9 all-gather.9
  201.2 109.0 all-gather.11
  312.4 95.1 all-gather.13
  419.8 67.1 reduce-scatter.1
where the time goes:
time: 503 us; the launch traced here: 501 us
  waiting for transfers between devices  382 us (76%)
  matrix products  74.2 us (15%)
  other arithmetic  17.9 us (4%)
  between operations  13.8 us (3%)
  starting transfers between devices  6.76 us (1%)
  local copies, waits for them, and re-layouts  6.07 us (1%)
    all_gather x1, waiting for transfers between devices, on_device(): pair_rows = lax.all_gather(tokens, 'fsdp', axis=0, tiled=True)  70.2 us
    reduce_scatter x1, waiting for transfers between devices, on_device(): lax.psum_scatter(partial_out.astype(jnp.bfloat16), 'fsdp', scatter_dimens...  67.3 us
    ppermute x2, waiting for transfers between devices, passed_along(): return lax.ppermute(block, axis, route)  65.5 us
    all_gather x1, waiting for transfers between devices, on_device(): lax.all_gather(key_matrix, 'seq', axis=0, tiled=True)  55.6 us
    all_gather x1, waiting for transfers between devices, on_device(): lax.all_gather(value_matrix, 'seq', axis=0, tiled=True)  49.6 us
    all_gather x1, waiting for transfers between devices, on_device(): lax.all_gather(out_weight, 'seq', axis=0, tiled=True)  46 us
    all_gather x1, waiting for transfers between devices, on_device(): lax.all_gather(query_weight, 'seq', axis=0, tiled=True)  24.8 us
    dot_general x1, matrix products, window_block(): jnp.einsum('kgrl,lkd->rkgd', weights, value_block, preferred_element_type...  14.2 us
  transfers between devices with their start and end apart: 8, of which 8 were waited for; matrix products, arithmetic and copies ran while one was open for 16% of the time, Pallas kernels for 0%

commit v1 on v0

--- a/solution.py
+++ b/solution.py
@@ -1,6 +1,10 @@
+import functools
+
 import jax
 import jax.numpy as jnp
 from jax import lax
+from jax.experimental import pallas as pl
+from jax.experimental.pallas import tpu as pltpu
 from jax.sharding import PartitionSpec as P
 
 HEAD_SIZE = 128
@@ -59,6 +63,159 @@
     return mixed.astype(jnp.bfloat16).reshape(query_block.shape[0], -1)
 
 
+def ring_place(chip, chips):
+    row, side = chip // 2, chip % 2
+    return side * (chips - 1 - row) + (1 - side) * row
+
+
+def ring_chip(place, chips):
+    back = place // (chips // 2)
+    return back * (2 * (chips - 1 - place) + 1) + (1 - back) * 2 * place
+
+
+def gather_kernel(
+    shards,
+    copies,
+    query_ref,
+    key_ref,
+    value_ref,
+    tokens_ref,
+    query_out,
+    key_out,
+    value_out,
+    tokens_out,
+    local_sem,
+    ring_send,
+    ring_recv,
+    pair_send,
+    pair_recv,
+    token_send,
+    token_recv,
+):
+    chips = shards // 2
+    me = lax.axis_index("seq")
+    group = lax.axis_index("fsdp")
+    core = me % 2
+    place = ring_place(me // 2, chips)
+    half = query_ref.shape[1] // 2
+    other = (me // 2) * 2 + 1 - core
+    ahead = ring_chip((place + 1) % chips, chips) * 2 + core
+    behind = ring_chip((place + chips - 1) % chips, chips) * 2 + core
+
+    barrier = pltpu.get_barrier_semaphore()
+    for device in (other, ahead, behind):
+        pl.semaphore_signal(
+            barrier, inc=1, device_id=(device, group), device_id_type=pl.DeviceIdType.MESH
+        )
+    for offset in range(1, copies):
+        pl.semaphore_signal(
+            barrier,
+            inc=1,
+            device_id=(me, (group + offset) % copies),
+            device_id_type=pl.DeviceIdType.MESH,
+        )
+    pl.semaphore_wait(barrier, 3 + copies - 1)
+
+    flows = (
+        (query_ref, query_out, 0, half, 1),
+        (key_ref, key_out, 0, key_ref.shape[1], -1),
+        (query_ref, query_out, half, half, 1),
+        (value_ref, value_out, 0, value_ref.shape[1], -1),
+    )
+    pending = []
+    arriving = []
+    token_slot = tokens_out.at[group]
+    ring_copies = {}
+    for step in range(chips):
+        for index, (source, target, column, width, way) in enumerate(flows):
+            columns = pl.ds(column, width)
+            owner = ring_chip((place - way * step + chips) % chips, chips) * 2 + core
+            slot = target.at[owner, :, columns]
+            if step == 0:
+                block = source.at[:, columns]
+            else:
+                block = slot
+                ring_copies[index, step - 1].wait_recv()
+            if step < chips - 1:
+                copy = pltpu.make_async_remote_copy(
+                    src_ref=block,
+                    dst_ref=slot,
+                    send_sem=ring_send.at[index, step],
+                    recv_sem=ring_recv.at[index, step],
+                    device_id=(ahead if way > 0 else behind, group),
+                    device_id_type=pl.DeviceIdType.MESH,
+                )
+                copy.start()
+                ring_copies[index, step] = copy
+                pending.append(copy)
+            across = pltpu.make_async_remote_copy(
+                src_ref=block,
+                dst_ref=slot,
+                send_sem=pair_send.at[index, step],
+                recv_sem=pair_recv.at[index, step],
+                device_id=(other, group),
+                device_id_type=pl.DeviceIdType.MESH,
+            )
+            across.start()
+            pending.append(across)
+            arriving.append(across)
+        if step == 0:
+            for offset in range(1, copies):
+                swap = pltpu.make_async_remote_copy(
+                    src_ref=tokens_ref,
+                    dst_ref=token_slot,
+                    send_sem=token_send.at[offset - 1],
+                    recv_sem=token_recv.at[offset - 1],
+                    device_id=(me, (group + offset) % copies),
+                    device_id_type=pl.DeviceIdType.MESH,
+                )
+                swap.start()
+                pending.append(swap)
+                arriving.append(swap)
+            local = [
+                pltpu.make_async_copy(query_ref, query_out.at[me], local_sem.at[0]),
+                pltpu.make_async_copy(key_ref, key_out.at[me], local_sem.at[1]),
+                pltpu.make_async_copy(value_ref, value_out.at[me], local_sem.at[2]),
+                pltpu.make_async_copy(tokens_ref, token_slot, local_sem.at[3]),
+            ]
+            for copy in local:
+                copy.start()
+    for copy in arriving:
+        copy.wait_recv()
+    for copy in pending:
+        copy.wait_send()
+    for copy in local:
+        copy.wait()
+
+
+def gathered(query_weight, key_matrix, value_matrix, tokens):
+    shards, copies = lax.axis_size("seq"), lax.axis_size("fsdp")
+    inputs = (query_weight, key_matrix, value_matrix, tokens)
+    counts = (shards, shards, shards, copies)
+    outputs = [
+        jax.ShapeDtypeStruct((n, *a.shape), a.dtype) for a, n in zip(inputs, counts)
+    ]
+    chips = shards // 2
+    anywhere = pl.BlockSpec(memory_space=pltpu.MemorySpace.HBM)
+    whole = pl.pallas_call(
+        functools.partial(gather_kernel, shards, copies),
+        out_shape=outputs,
+        in_specs=[anywhere] * 4,
+        out_specs=[anywhere] * 4,
+        scratch_shapes=[
+            pltpu.SemaphoreType.DMA((4,)),
+            pltpu.SemaphoreType.DMA((4, chips)),
+            pltpu.SemaphoreType.DMA((4, chips)),
+            pltpu.SemaphoreType.DMA((4, chips)),
+            pltpu.SemaphoreType.DMA((4, chips)),
+            pltpu.SemaphoreType.DMA((copies,)),
+            pltpu.SemaphoreType.DMA((copies,)),
+        ],
+        compiler_params=pltpu.CompilerParams(collective_id=0, has_side_effects=True),
+    )(*inputs)
+    return [a.reshape(-1, a.shape[-1]) for a in whole]
+
+
 def on_device(
     tokens,
     norm_gain,
@@ -70,7 +227,11 @@
     key_gain,
     post_gain,
 ):
-    pair_rows = lax.all_gather(tokens, "fsdp", axis=0, tiled=True)
+    query_full, key_full, value_full, pair_rows = gathered(
+        query_weight, key_matrix, value_matrix, tokens
+    )
+    out_weight, pair_rows = lax.optimization_barrier((out_weight, pair_rows))
+    out_full = lax.all_gather(out_weight, "seq", axis=0, tiled=True)
     shard_rows = pair_rows.shape[0]
     first_row = lax.axis_index("seq") * shard_rows
     normed_input = rms_scaled(pair_rows.astype(jnp.float32), norm_gain).astype(jnp.bfloat16)
@@ -78,15 +239,9 @@
     key_width = key_matrix.shape[1]
     local_heads = key_width // HEAD_SIZE
     query_groups = query_width // key_width
-    query_full, key_full, value_full, out_full = (
-        lax.all_gather(query_weight, "seq", axis=0, tiled=True),
-        lax.all_gather(key_matrix, "seq", axis=0, tiled=True),
-        lax.all_gather(value_matrix, "seq", axis=0, tiled=True),
-        lax.all_gather(out_weight, "seq", axis=0, tiled=True),
-    )
-    queries_raw = jnp.dot(normed_input, query_full, preferred_element_type=jnp.float32)
     keys_raw = jnp.dot(normed_input, key_full, preferred_element_type=jnp.float32)
     values_raw = jnp.dot(normed_input, value_full, preferred_element_type=jnp.float32)
+    queries_raw = jnp.dot(normed_input, query_full, preferred_element_type=jnp.float32)
     positions = first_row + jnp.arange(shard_rows, dtype=jnp.int32)
     query_states = head_states(queries_raw, query_gain, positions).reshape(
         shard_rows, local_heads, query_groups, HEAD_SIZE
@@ -100,17 +255,31 @@
     for distance in range(1, count + 1):
         received = [passed_along(stacked, "seq", distance)] + received
     window_rows = jnp.concatenate(received + [stacked], axis=1)
-    key_rows = window_rows.shape[1]
-    keys_window = window_rows[0].reshape(key_rows, local_heads, HEAD_SIZE)
-    values_window = window_rows[1].reshape(key_rows, local_heads, HEAD_SIZE)
-    key_pos = first_row - WINDOW_LENGTH + jnp.arange(key_rows, dtype=jnp.int32)
-    attended = window_block(query_states, keys_window, values_window, positions, key_pos)
-    partial_out = lax.dot_general(
-        attended, out_full, (((1,), (1,)), ((), ())), preferred_element_type=jnp.float32
-    )
-    summed = lax.psum_scatter(
-        partial_out.astype(jnp.bfloat16), "fsdp", scatter_dimension=0, tiled=True
-    ).astype(jnp.float32)
+    copies = lax.axis_size("fsdp")
+    group = lax.axis_index("fsdp")
+    part_rows = shard_rows // copies
+    part_keys = window_rows.shape[1] - shard_rows + part_rows
+
+    def partial_rows(part, states):
+        begin = part * part_rows
+        queries = lax.dynamic_slice_in_dim(states, begin, part_rows, 0)
+        window = lax.dynamic_slice_in_dim(window_rows, begin, part_keys, 1)
+        keys = window[0].reshape(part_keys, local_heads, HEAD_SIZE)
+        values = window[1].reshape(part_keys, local_heads, HEAD_SIZE)
+        query_pos = first_row + begin + jnp.arange(part_rows, dtype=jnp.int32)
+        key_pos = first_row + begin - WINDOW_LENGTH + jnp.arange(part_keys, dtype=jnp.int32)
+        attended = window_block(queries, keys, values, query_pos, key_pos)
+        return lax.dot_general(
+            attended, out_full, (((1,), (1,)), ((), ())), preferred_element_type=jnp.float32
+        ).astype(jnp.bfloat16)
+
+    summed = 0.0
+    for offset in range(1, copies):
+        away = partial_rows((group + offset) % copies, query_states)
+        route = [(i, (i + offset) % copies) for i in range(copies)]
+        query_states, away = lax.optimization_barrier((query_states, away))
+        summed = summed + lax.ppermute(away, "fsdp", route).astype(jnp.float32)
+    summed = partial_rows(group, query_states).astype(jnp.float32) + summed
     return (tokens.astype(jnp.float32) + rms_scaled(summed, post_gain)).astype(jnp.bfloat16)
 
 

time: 503 us -> 349 us (0.69); the launches traced: 501 us -> 342 us
  waiting for transfers between devices: 382 us -> 72.3 us
  Pallas kernels: 0 us -> 129 us
  local copies, waits for them, and re-layouts: 6.07 us -> 35.4 us
  matrix products: 74.2 us -> 63.9 us
    all_gather x5 -> x1, waiting for transfers between devices: 246 us -> 0.01 us  [on_device(): out_full = lax.all_gather(out_weight, 'seq', axis=0, tiled=True)]
    pallas_call x0 -> x1, Pallas kernels: none -> 129 us  [gathered(): pl.pallas_call(functools.partial(gather_kernel, shards, copies), out_shap...]
    reduce_scatter x1 -> x0, waiting for transfers between devices: 67.3 us -> none  [on_device(): lax.psum_scatter(partial_out.astype(jnp.bfloat16), 'fsdp', scatter_dimens...]
    ppermute x0 -> x1, waiting for transfers between devices: none -> 42 us  [on_device(): summed = summed + lax.ppermute(away, 'fsdp', route).astype(jnp.float32)]
    ppermute x2, waiting for transfers between devices: 65.5 us -> 30.3 us  [passed_along(): return lax.ppermute(block, axis, route)]
    dot_general x0 -> x2, local copies, waits for them, and re-layouts: none -> 22.5 us  [the longest x1 14.2 us: on_device(): jnp.dot(normed_input, query_full, preferred_element_type=jnp.float32)]
    dot_general x2, matrix products: 24 us -> 17.4 us  [partial_rows(): lax.dot_general(attended, out_full, (((1,), (1,)), ((), ())), preferred_e...]
    dot_general x1 -> x2, matrix products: 14.2 us -> 13.5 us  [window_block(): jnp.einsum('kgrl,lkd->rkgd', weights, value_block, preferred_element_type...]
  transfers between devices with their start and end apart: 8 -> 4, of which waited for: 8 -> 2; matrix products, arithmetic and copies ran while one was open for 16% -> 28% of each run, Pallas kernels for 0% -> 0%
where the time goes in v1:
time: 349 us; the launch traced here: 342 us
  Pallas kernels  129 us (37%)
  waiting for transfers between devices  72.3 us (21%)
  matrix products  63.9 us (18%)
  local copies, waits for them, and re-layouts  35.4 us (10%)
  other arithmetic  18.9 us (5%)
  between operations  14.2 us (4%)
  starting transfers between devices  8.24 us (2%)
    pallas_call x1, Pallas kernels, gathered(): pl.pallas_call(functools.partial(gather_kernel, shards, copies), out_shap...  129 us
    ppermute x1, waiting for transfers between devices, on_device(): summed = summed + lax.ppermute(away, 'fsdp', route).astype(jnp.float32)  42 us
    ppermute x2, waiting for transfers between devices, passed_along(): return lax.ppermute(block, axis, route)  30.3 us
    dot_general x2, matrix products, partial_rows(): lax.dot_general(attended, out_full, (((1,), (1,)), ((), ())), preferred_e...  17.4 us
    dot_general x1, local copies, waits for them, and re-layouts, on_device(): jnp.dot(normed_input, query_full, preferred_element_type=jnp.float32)  14.2 us
    dot_general x2, matrix products, window_block(): jnp.einsum('kgrl,lkd->rkgd', weights, value_block, preferred_element_type...  13.5 us
    dot_general x1, matrix products, on_device(): jnp.dot(normed_input, query_full, preferred_element_type=jnp.float32)  10.5 us
    sub x2, matrix products, window_block(): raised = jnp.exp(scores - highest)  9.79 us
  transfers between devices with their start and end apart: 4, of which 2 were waited for; matrix products, arithmetic and copies ran while one was open for 28% of the time, Pallas kernels for 0%

profile of v1, /device:TPU:5, one launch (start us, length us, event | category | flops | bytes accessed | tf_op | source)
XLA Modules:
  0.0 341.6 jit_solution(12876229470253224511)
XLA Ops:
  6.5 0.0 all-gather.2.cloned.1.call-start
  6.5 128.7 %shard_map.91 = (bf16[16,336,1024]{2,1,0:T(8,128)(2,1)}, bf16[16,336,512]{2,1,0:T(8,128)(2,1)}, bf16[16,336,512]{2,1,0:T(8,128)(2,1)}, bf16[2,256,5376]{2,1,0:T(8,128)(2,1)}) custom-call(bf16[336,1024]{1,0:T(8,128)(2,1)} %query_ref.1, bf16[336,512]{1,0:T(8,128)(2,1)} %key_ref.1, bf16[336,512]{1,0:T(8,128)(2,1)} %value_ref.1, bf16[256,5376]{1,0:T(8,128)(2,1)} %tokens_ref.1), custom_call_target="tpu_custom_call" | custom-call | tf_op jit(solution)/shard_map/pallas_call | solution.py:200
  135.2 0.0 all-gather.2.cloned.1.call-update
  135.3 0.0 copy-start.7
  135.3 8.3 %copy.10 = bf16[512,5376]{1,0:T(8,128)(2,1)} copy(bf16[512,5376]{0,1:T(8,128)(2,1)} %bitcast.81) | data formatting | bytes 11010048 | tf_op jit(solution)/shard_map/dot_general | solution.py:242
  143.6 4.3 %fusion.2 = f32[512]{0:T(512)S(1)} fusion(bf16[512,5376]{1,0:T(8,128)(2,1)} %bitcast.77), kind=kLoop, calls=%fused_computation.4 | loop fusion | flops 8257024 | bytes 5507072 | tf_op jit(solution)/shard_map/reduce_sum | solution.py:27
  147.9 0.0 copy-done.7
  147.9 0.3 copy-done.1
  148.3 5.4 %multiply_reduce_fusion.2 = (f32[512,4]{0,1:T(4,128)S(1)}, f32[512,4,128]{0,2,1:T(8,128)S(1)}) fusion(bf16[4,128,5376]{2,1,0:T(8,128)(2,1)S(1)} %bitcast.82, f32[5376]{0:T(1024)S(1)} %copy-done.7, f32[512]{0:T(512)S(1)} %add_rsqrt_fusion.2, bf16[512,5376]{1,0:T(8,128)(2,1)} %bitcast.78), kind=kOutput, calls=%fused_computation.56 | convolution fusion | flops 2830104576 | bytes 12090368 | tf_op jit(solution)/shard_map/dot_general | solution.py:242
  153.7 0.5 multiply_cosine_fusion
  154.2 0.0 copy-done.5
  154.3 0.2 multiply_multiply_fusion.1
  154.5 0.2 subtract_convert_fusion.1
  154.7 0.2 copy.11
  154.9 7.3 %fusion.30 = bf16[1,512,512]{2,1,0:T(8,128)(2,1)S(1)} fusion(bf16[5376,512]{1,0:T(8,128)(2,1)} %bitcast.92, bf16[512,5376]{1,0:T(8,128)(2,1)} %bitcast.79, f32[5376]{0:T(1024)S(1)} %copy-done.7, f32[512]{0:T(512)S(1)} %add_rsqrt_fusion.2), kind=kOutput, calls=%fused_computation.51 | convolution fusion | flops 2829844480 | bytes 11557888 | tf_op jit(solution)/shard_map/dot_general | solution.py:243
  162.2 1.1 pad_maximum_fusion
  163.3 3.8 %collective-permute-start.1 = (bf16[2,512,512]{2,1,0:T(8,128)(2,1)}, bf16[2,512,512]{2,1,0:T(8,128)(2,1)}, u32[]{:S(2)}, u32[]{:S(2)}) collective-permute-start(bf16[2,512,512]{2,1,0:T(8,128)(2,1)} %pad_maximum_fusion), channel_id=1, source_target_pairs={{0,2},{2,4},{4,6},{6,8},{8,10},{10,12},{12,14},{14,16},{16,18},{18... | collective-permute-start | bytes 3145736 | tf_op jit(solution)/shard_map/ppermute | solution.py:23
  167.1 3.3 collective-permute-start
  170.4 14.2 %copy.12 = bf16[1024,5376]{1,0:T(8,128)(2,1)} copy(bf16[1024,5376]{0,1:T(8,128)(2,1)} %bitcast.75) | data formatting | bytes 22020096 | tf_op jit(solution)/shard_map/dot_general | solution.py:244
  184.6 10.5 %multiply_reduce_fusion.1 = (f32[512,8]{0,1:T(8,128)S(1)}, f32[512,8,128]{0,2,1:T(8,128)S(1)}) fusion(bf16[8,128,5376]{2,1,0:T(8,128)(2,1)} %bitcast.76, f32[5376]{0:T(1024)S(1)} %copy-done.7, f32[512]{0:T(512)S(1)} %add_rsqrt_fusion.2, bf16[512,5376]{1,0:T(8,128)(2,1)} %bitcast.80), kind=kOutput, calls=%fused_computation.35 | convolution fusion | flops 5649199104 | bytes 18652160 | tf_op jit(solution)/shard_map/dot_general | solution.py:244
  195.1 0.0 copy-done.6
  195.1 0.5 multiply_multiply_fusion
  195.6 1.2 subtract_convert_fusion
  196.8 0.5 copy.14
  197.3 1.5 copy.13
  198.8 1.1 fusion.39
  200.0 1.6 pad_maximum_fusion.1
  201.6 0.9 fusion.27
  202.5 0.0 collective-permute-done.1
  202.5 30.3 %collective-permute-done = bf16[2,512,512]{2,1,0:T(8,128)(2,1)} collective-permute-done((bf16[2,512,512]{2,1,0:T(8,128)(2,1)}, bf16[2,512,512]{2,1,0:T(8,128)(2,1)}, u32[]{:S(2)}, u32[]{:S(2)}) %collective-permute-start) | collective-permute-done | bytes 1048608 | tf_op jit(solution)/shard_map/ppermute | solution.py:23
  232.8 1.7 maximum_maximum_fusion
  234.5 0.0 copy-start.3
  234.5 2.1 constant_dynamic-slice_fusion.2
  236.6 2.4 copy.30
  239.1 3.8 %reshape_squeeze.15 = bf16[1280,4,128]{2,1,0:T(4,128)(2,1)} reshape(bf16[1,1280,512]{2,1,0:T(8,128)(2,1)} %get-tuple-element.21) | data formatting | bytes 2621440 | tf_op jit(solution)/shard_map/reshape;squeeze | solution.py:267
  242.8 5.0 %fusion.84 = f32[4,2,256]{2,1,0:T(2,128)S(1)} fusion(pred[256,1280]{0,1:T(8,128)(4,1)S(1)} %fusion.27, bf16[256,4,2,128]{3,0,2,1:T(8,128)(2,1)S(1)} %copy-done.3, bf16[1280,4,128,1]{2,1,0,3:T(4,128)(2,1)} %bitcast.90), kind=kOutput, calls=%fused_computation.97 | convolution fusion | flops 681575680 | bytes 2170880 | tf_op jit(solution)/shard_map/sub | solution.py:60
  247.8 7.5 %fusion.29 = bf16[4,128,2,256]{3,1,2,0:T(8,128)(2,1)} fusion(bf16[1280,4,128,1]{0,2,3,1:T(8,128)(2,1)} %bitcast.87, f32[4,2,256]{2,1,0:T(2,128)S(1)} %fusion.84, pred[256,1280]{0,1:T(8,128)(4,1)S(1)} %fusion.27, bf16[256,4,2,128]{3,0,2,1:T(8,128)(2,1)S(1)} %copy-done.3, bf16[1280,4,128,1]{2,1,0,3:T(4,128)(2,1)} %bitcast.91), kind=kOutput, calls=%fused_computation.50 | convolution fusion | flops 1355549952 | bytes 4005888 | tf_op jit(solution)/shard_map/kgrl,lkd->rkgd/dot_general | solution.py:62
  255.3 8.9 %convolution_convert_fusion.1 = bf16[256,5376]{1,0:T(8,128)(2,1)} fusion(bf16[256,1024]{0,1:T(8,128)(2,1)} %bitcast.94, bf16[5376,1024]{1,0:T(8,128)(2,1)} %all-gather.2.cloned.1.call-done), kind=kOutput, calls=%fused_computation.17 | convolution fusion | flops 2819948544 | bytes 14286848 | tf_op jit(solution)/shard_map/dot_general | solution.py:272
  264.2 1.1 collective-permute-start.2
  265.4 1.0 fusion.25
  266.4 1.5 copy.27
  267.8 0.6 reshape_squeeze.13
  268.4 0.0 copy-start.2
  268.4 4.8 %fusion.87 = f32[4,2,256]{2,1,0:T(2,128)S(1)} fusion(pred[256,1280]{0,1:T(8,128)(4,1)S(1)} %fusion.25, bf16[1280,4,128,1]{2,1,0,3:T(4,128)(2,1)S(1)} %bitcast.88, bf16[512,4,2,128]{3,0,2,1:T(8,128)(2,1)} %pad_maximum_fusion.1, s32[]{:T(128)S(6)} %select_n.31), kind=kOutput, calls=%fused_computation.98 | convolution fusion | flops 681575680 | bytes 2170884 | tf_op jit(solution)/shard_map/sub | solution.py:60
  273.3 6.0 %fusion.28 = bf16[4,128,2,256]{3,1,2,0:T(8,128)(2,1)S(1)} fusion(bf16[1280,4,128,1]{0,2,3,1:T(8,128)(2,1)S(1)} %bitcast.86, f32[4,2,256]{2,1,0:T(2,128)S(1)} %fusion.87, pred[256,1280]{0,1:T(8,128)(4,1)S(1)} %fusion.25, bf16[1280,4,128,1]{2,1,0,3:T(4,128)(2,1)S(1)} %bitcast.89, bf16[512,4,2,128]{3,0,2,1:T(8,128)(2,1)} %pad_maximum_fusion.1, s32[]{:T(128)S(6)} %select_n.31), kind=kOutput, calls=%fused_computation.49 | convolution fusion | flops 1355549952 | bytes 4005892 | tf_op jit(solution)/shard_map/kgrl,lkd->rkgd/dot_general | solution.py:62
  279.3 42.0 %collective-permute-done.2 = bf16[256,5376]{1,0:T(8,128)(2,1)} collective-permute-done((bf16[256,5376]{1,0:T(8,128)(2,1)}, bf16[256,5376]{1,0:T(8,128)(2,1)}, u32[]{:S(2)}, u32[]{:S(2)}) %collective-permute-start.2) | collective-permute-done | bytes 2752544 | tf_op jit(solution)/shard_map/ppermute | solution.py:281
  321.3 8.5 %multiply_reduce_fusion = (f32[256]{0:T(256)S(1)}, f32[256,5376]{1,0:T(8,128)S(1)}) fusion(bf16[256,5376]{1,0:T(8,128)(2,1)} %collective-permute-done.2, bf16[256,1024]{0,1:T(8,128)(2,1)S(1)} %bitcast.93, bf16[5376,1024]{1,0:T(8,128)(2,1)} %all-gather.2.cloned.1.call-done), kind=kOutput, calls=%fused_computation.23 | convolution fusion | flops 2826829568 | bytes 19792896 | tf_op jit(solution)/shard_map/dot_general | solution.py:272
  329.8 4.5 %add_convert_fusion = bf16[256,5376]{1,0:T(8,128)(2,1)} fusion(bf16[256,5376]{1,0:T(8,128)(2,1)S(1)} %copy-done, f32[256,5376]{1,0:T(8,128)S(1)} %get-tuple-element.36, bf16[256,5376]{1,0:T(8,128)(2,1)} %collective-permute-done.2, f32[5376]{0:T(1024)S(1)} %copy-done.4, f32[256]{0:T(256)S(1)} %add_rsqrt_fusion.3), kind=kLoop, calls=%fused_computation.22 | loop fusion | flops 9633792 | bytes 13785088 | tf_op jit(solution)/shard_map/convert_element_type | solution.py:283
  (23 shorter events, 0.1 us)
Async XLA Ops:
  6.5 248.8 %all-gather.2.cloned.1.call-start = ((), (), s32[]{:S(2)}) async-start(), calls=%async_computation | async-start | bytes 11698176 | tf_op jit(solution)/shard_map/all_gather | solution.py:234
  135.3 12.7 %copy-start.7 = (f32[5376]{0:T(1024)S(1)}, f32[5376]{0:T(1024)}, u32[]{:S(2)}) copy-start(f32[5376]{0:T(1024)} %param.10) | copy-start | bytes 64516
  143.6 4.7 %copy-start.1 = (bf16[512,5376]{1,0:T(8,128)(2,1)S(1)}, bf16[512,5376]{1,0:T(8,128)(2,1)}, u32[]{:S(2)}) copy-start(bf16[512,5376]{1,0:T(8,128)(2,1)} %copy.10) | copy-start | bytes 16515076
  148.3 6.0 %copy-start.5 = (f32[128]{0:T(128)S(1)}, f32[128]{0:T(128)}, u32[]{:S(2)}) copy-start(f32[128]{0:T(128)} %param.16) | copy-start | bytes 1540
  163.3 39.2 %collective-permute-start.1 = (bf16[2,512,512]{2,1,0:T(8,128)(2,1)}, bf16[2,512,512]{2,1,0:T(8,128)(2,1)}, u32[]{:S(2)}, u32[]{:S(2)}) collective-permute-start(bf16[2,512,512]{2,1,0:T(8,128)(2,1)} %pad_maximum_fusion), channel_id=1, source_target_pairs={{0,2},{2,4},{4,6},{6,8},{8,10},{10,12},{12,14},{14,16},{16,18},{18... | collective-permute-start | bytes 3145736 | tf_op jit(solution)/shard_map/ppermute | solution.py:23
  167.1 65.8 %collective-permute-start = (bf16[2,512,512]{2,1,0:T(8,128)(2,1)}, bf16[2,512,512]{2,1,0:T(8,128)(2,1)}, u32[]{:S(2)}, u32[]{:S(2)}) collective-permute-start(bf16[2,512,512]{2,1,0:T(8,128)(2,1)} %pad_maximum_fusion), channel_id=1, source_target_pairs={{0,4},{2,6},{4,8},{6,10},{8,12},{10,14},{12,16},{14,18},{16,20},{1... | collective-permute-start | bytes 3145736 | tf_op jit(solution)/shard_map/ppermute | solution.py:23
  184.6 10.5 %copy-start.6 = (f32[128]{0:T(128)S(1)}, f32[128]{0:T(128)}, u32[]{:S(2)}) copy-start(f32[128]{0:T(128)} %param.15) | copy-start | bytes 1540
  234.5 8.3 %copy-start.3 = (bf16[256,4,2,128]{3,0,2,1:T(8,128)(2,1)S(1)}, bf16[256,4,2,128]{3,0,2,1:T(8,128)(2,1)}, u32[]{:S(2)}) copy-start(bf16[256,4,2,128]{3,0,2,1:T(8,128)(2,1)} %fusion.39) | copy-start | bytes 1572868
  264.2 57.1 %collective-permute-start.2 = (bf16[256,5376]{1,0:T(8,128)(2,1)}, bf16[256,5376]{1,0:T(8,128)(2,1)}, u32[]{:S(2)}, u32[]{:S(2)}) collective-permute-start(bf16[256,5376]{1,0:T(8,128)(2,1)} %convolution_convert_fusion.1), channel_id=1, source_target_pairs={{0,1},{1,0},{2,3},{3,2},{4,5},{5,4},{6,7},{7,6},{8,9},{9,8},{10,11... | collective-permute-start | bytes 8257544 | tf_op jit(solution)/shard_map/ppermute | solution.py:281
  268.4 4.8 %copy-start.2 = (bf16[1,1280,512]{1,2,0:T(8,128)(2,1)S(1)}, bf16[1,1280,512]{1,2,0:T(8,128)(2,1)}, u32[]{:S(2)}) copy-start(bf16[1,1280,512]{1,2,0:T(8,128)(2,1)} %copy.27) | copy-start | bytes 3932164
  321.3 8.5 %copy-start = (bf16[256,5376]{1,0:T(8,128)(2,1)S(1)}, bf16[256,5376]{1,0:T(8,128)(2,1)}, u32[]{:S(2)}) copy-start(bf16[256,5376]{1,0:T(8,128)(2,1)} %tokens_ref.1) | copy-start | bytes 8257540
  321.3 8.5 %copy-start.4 = (f32[5376]{0:T(1024)S(1)}, f32[5376]{0:T(1024)}, u32[]{:S(2)}) copy-start(f32[5376]{0:T(1024)} %param.17) | copy-start | bytes 64516
Sparse Core Ops, SparseCore 0:
  135.4 114.5 all-gather.1
